TPU v7x, 32 devices: a whole 2x2x4 slice. The times are simulated.
32 devices in a mesh: row: 8 (over z, x), col: 4 (over y, core).
Axes of the slice: x: 2, y: 2, z: 4, core: 2. Of those that a mesh axis runs over, the one named last changes fastest.
Arguments:
- snapshot: bfloat16 [512, 256, 512], P('row', 'col'), may hold values from -6 to 6
- basis_two: bfloat16 [256, 128], P('col'), may hold values from -0.375 to 0.375
- basis_three: bfloat16 [512, 128], replicated, may hold values from -0.25 to 0.25
Outputs:
- gram: float32 [512, 512], P('row', 'col')
All inputs are finite; a program needn't handle non-finite values.
Results may differ from a plain program's by a relative error of at most 0.0017.
Values may be sent and summed in bfloat16 or wider, within the bound.
No kernel may reach another device: no remote copies, remote signals or barrier semaphores. Data moves between devices by JAX's collectives and lax.ppermute only.
A program may use at most 64 MiB of HBM per device.

v0:
```python
import jax
import jax.numpy as jnp
from jax import lax
from jax.sharding import PartitionSpec as P


def on_device(snapshot, basis_two, basis_three):
    cells_one, cells_two, cells_three = snapshot.shape
    ranks_two = basis_two.shape[1]
    ranks_three = basis_three.shape[1]
    inner = jnp.dot(
        snapshot.reshape(cells_one * cells_two, cells_three),
        basis_three,
        preferred_element_type=jnp.float32,
    )
    inner = inner.astype(jnp.bfloat16).reshape(cells_one, cells_two, ranks_three)
    regrouped = lax.all_to_all(inner, "col", split_axis=2, concat_axis=1, tiled=True)
    whole_factor = lax.all_gather(basis_two, "col", axis=0, tiled=True)
    full = jnp.einsum("abr,bq->qar", regrouped, whole_factor, preferred_element_type=jnp.float32)
    rounded = lax.all_to_all(
        full.astype(jnp.bfloat16), "col", split_axis=0, concat_axis=2, tiled=True
    )
    partial_gram = jnp.einsum(
        "qar,qbr->ab",
        rounded,
        lax.all_gather(rounded, "row", axis=1, tiled=True),
        preferred_element_type=jnp.float32,
    )
    summed_gram = lax.psum_scatter(partial_gram, "col", scatter_dimension=1, tiled=True)
    return summed_gram * (1.0 / (ranks_two * ranks_three))


def solution(mesh):
    in_specs = (P("row", "col", None), P("col", None), P())
    out_specs = P("row", "col")
    return jax.shard_map(
        on_device, mesh=mesh, in_specs=in_specs, out_specs=out_specs, check_vma=False
    )
```

profile of v0, /device:TPU:0, one launch (start us, length us, event | category | flops | bytes accessed | tf_op | source)
XLA Modules:
  0.0 165.3 jit_solution(16451007527104671222)
XLA Ops:
  6.5 0.9 copy-done
  7.4 3.4 %convolution_convert_fusion = bf16[4096,128]{1,0:T(8,128)(2,1)S(1)} fusion(bf16[4096,512]{1,0:T(8,128)(2,1)} %bitcast.31, bf16[512,128]{1,0:T(8,128)(2,1)S(1)} %copy-done), kind=kOutput, calls=%fused_computation | convolution fusion | flops 537395200 | bytes 5373952 | tf_op jit(solution)/shard_map/dot_general | solution.py:11
  10.9 0.0 copy-start.1
  10.9 3.0 %copy.20 = bf16[64,64,128]{1,0,2:T(8,128)(2,1)S(1)} copy(bf16[64,64,128]{2,1,0:T(8,128)(2,1)S(1)} %bitcast.32) | data formatting | bytes 2097152 | tf_op jit(solution)/shard_map/reshape | solution.py:16
  13.9 2.6 %reshape.10 = bf16[4,2,65536]{2,1,0:T(2,128)(2,1)} reshape(bf16[128,64,64]{2,1,0:T(8,128)(2,1)S(1)} %bitcast.29) | data formatting | bytes 2097152
  16.5 4.3 %all-to-all-start = ((bf16[4,2,65536]{2,1,0:T(2,128)(2,1)}), bf16[4,2,65536]{2,1,0:T(2,128)(2,1)S(1)}, u32[]{:S(2)}, u32[]{:S(2)}) async-start(bf16[4,2,65536]{2,1,0:T(2,128)(2,1)} %reshape.10), calls=%async_computation | async-start | bytes 2097152 | tf_op jit(solution)/shard_map/all_to_all | solution.py:17
  20.8 15.6 %all_gather.6 = bf16[256,128]{1,0:T(8,128)(2,1)S(1)} all-gather(bf16[64,128]{1,0:T(8,128)(2,1)S(1)} %copy-done.1), channel_id=1, replica_groups=mesh['row'=8,'col'=4] {'col'}, dimensions={0}, use_global_device_ids=true | all-gather | bytes 81920 | tf_op jit(solution)/shard_map/all_gather | solution.py:18
  36.4 1.4 reshape.11
  37.8 3.0 %copy.22 = bf16[64,4,64,32]{2,1,3,0:T(4,128)(2,1)} copy(bf16[64,4,64,32]{2,0,3,1:T(8,128)(2,1)S(1)} %bitcast.30) | data formatting | bytes 2097152 | tf_op jit(solution)/shard_map/all_to_all | solution.py:17
  40.8 3.5 %all_to_all.29 = bf16[64,256,32]{1,2,0:T(8,128)(2,1)S(1)} reshape(bf16[64,4,64,32]{2,1,3,0:T(4,128)(2,1)} %copy.22) | data formatting | bytes 2097152 | tf_op jit(solution)/shard_map/all_to_all | solution.py:17
  44.3 0.4 fusion
  44.7 1.7 %copy.23 = bf16[128,64,32]{1,2,0:T(8,128)(2,1)S(1)} copy(bf16[128,64,32]{0,2,1:T(8,128)(2,1)S(1)} %fusion) | data formatting | bytes 1048576 | tf_op jit(solution)/shard_map/convert_element_type | solution.py:21
  46.4 0.9 reshape.12
  47.3 11.2 %all_to_all.36 = bf16[4,2,32768]{2,1,0:T(2,128)(2,1)S(1)} all-to-all(bf16[4,2,32768]{2,1,0:T(2,128)(2,1)S(1)} %reshape.12), channel_id=1, replica_groups=mesh['row'=8,'col'=4] {'col'}, dimensions={0} | all-to-all | bytes 1048576 | tf_op jit(solution)/shard_map/all_to_all | solution.py:20
  58.5 0.7 reshape.13
  59.2 0.1 copy.24
  59.4 1.1 copy.25
  60.5 0.0 all-gather.2.cloned.1.call-update
  60.5 0.0 reduce-scatter.2.cloned.1.call-start
  60.6 73.9 %all-gather.2.cloned.1.call-done = bf16[32,512,128]{2,1,0:T(8,128)(2,1)} async-done(((bf16[32,64,128]{2,1,0:T(8,128)(2,1)}), bf16[32,512,128]{2,1,0:T(8,128)(2,1)}) %all-gather.2.cloned.1.call-update) | async-done | bytes 4194320 | tf_op jit(solution)/shard_map/all_gather | solution.py:26
  134.4 4.2 %convolution_bitcast_fusion = f32[64,512]{1,0:T(8,128)} fusion(bf16[32,64,128]{1,2,0:T(8,128)(2,1)S(1)} %bitcast.28, bf16[32,512,128]{2,1,0:T(8,128)(2,1)} %all-gather.2.cloned.1.call-done), kind=kOutput, calls=%fused_computation.3 | convolution fusion | flops 268435456 | bytes 4849664 | tf_op jit(solution)/shard_map/qar,qbr->ab/dot_general | solution.py:23
  138.7 0.0 reduce-scatter.2.cloned.1.call-update
  138.7 18.3 %reduce-scatter.2.cloned.1.call-done = f32[64,128]{1,0:T(8,128)} async-done(((f32[64,512]{1,0:T(8,128)}), f32[64,128]{1,0:T(8,128)}) %reduce-scatter.2.cloned.1.call-update) | async-done | bytes 32784 | tf_op jit(solution)/shard_map/reduce_scatter | solution.py:29
  157.0 1.4 broadcast_multiply_fusion
  (4 shorter events, 0.0 us)
Async XLA Ops:
  6.5 0.9 copy-start
  10.9 9.9 %copy-start.1 = (bf16[64,128]{1,0:T(8,128)(2,1)S(1)}, bf16[64,128]{1,0:T(8,128)(2,1)}, u32[]{:S(2)}) copy-start(bf16[64,128]{1,0:T(8,128)(2,1)} %param.4) | copy-start | bytes 49156
  16.5 19.9 %all-to-all-start = ((bf16[4,2,65536]{2,1,0:T(2,128)(2,1)}), bf16[4,2,65536]{2,1,0:T(2,128)(2,1)S(1)}, u32[]{:S(2)}, u32[]{:S(2)}) async-start(bf16[4,2,65536]{2,1,0:T(2,128)(2,1)} %reshape.10), calls=%async_computation | async-start | bytes 2097152 | tf_op jit(solution)/shard_map/all_to_all | solution.py:17
  20.8 113.7 %all-gather.2.cloned.1.call-start = ((), (), s32[]{:S(2)}) async-start(), calls=%async_computation.3 | async-start | bytes 4718592 | tf_op jit(solution)/shard_map/all_gather | solution.py:26
  60.5 96.5 %reduce-scatter.2.cloned.1.call-start = ((), (), s32[]{:S(2)}) async-start(), calls=%async_computation.4 | async-start | bytes 163840 | tf_op jit(solution)/shard_map/reduce_scatter | solution.py:29
Sparse Core Ops, SparseCore 0:
  60.6 73.7 all-gather.1
  138.8 18.1 reduce-scatter.1
where the time goes:
time: 166 us; the launch traced here: 165 us
  waiting for transfers between devices  92.3 us (56%)
  blocking collectives  26.8 us (16%)
  local copies, waits for them, and re-layouts  18.9 us (11%)
  between operations  13.5 us (8%)
  matrix products  8.09 us (5%)
  starting transfers between devices  4.3 us (3%)
    all_gather x1, waiting for transfers between devices, on_device(): lax.all_gather(rounded, 'row', axis=1, tiled=True)  73.9 us
    reduce_scatter x1, waiting for transfers between devices, on_device(): lax.psum_scatter(partial_gram, 'col', scatter_dimension=1, tiled=True)  18.3 us
    all_gather x1, blocking collectives, on_device(): whole_factor = lax.all_gather(basis_two, 'col', axis=0, tiled=True)  15.6 us
    all_to_all x1, blocking collectives, on_device(): lax.all_to_all(full.astype(jnp.bfloat16), 'col', split_axis=0, concat_axi...  11.2 us
    unnamed x8, local copies, waits for them, and re-layouts  6.55 us
    all_to_all x2, local copies, waits for them, and re-layouts, on_device(): lax.all_to_all(inner, 'col', split_axis=2, concat_axis=1, tiled=True)  6.45 us
    all_to_all x1, starting transfers between devices, on_device(): lax.all_to_all(inner, 'col', split_axis=2, concat_axis=1, tiled=True)  4.26 us
    dot_general x1, matrix products, on_device(): jnp.einsum('qar,qbr->ab', rounded, lax.all_gather(rounded, 'row', axis=1,...  4.22 us
  transfers between devices with their start and end apart: 3, of which 2 were waited for; matrix products, arithmetic and copies ran while one was open for 0% of the time, Pallas kernels for 0%

commit v1 on v0

--- a/solution.py
+++ b/solution.py
@@ -23,7 +23,7 @@
     partial_gram = jnp.einsum(
         "qar,qbr->ab",
         rounded,
-        lax.all_gather(rounded, "row", axis=1, tiled=True),
+        jnp.concatenate(lax.all_gather(rounded, "row"), axis=1),
         preferred_element_type=jnp.float32,
     )
     summed_gram = lax.psum_scatter(partial_gram, "col", scatter_dimension=1, tiled=True)

time: 166 us -> 167 us (level)
  local copies, waits for them, and re-layouts: 18.9 us -> 22.1 us
  matrix products: 8.09 us -> 5.93 us
    reshape x0 -> x1, local copies, waits for them, and re-layouts: none -> 3.15 us  [on_device(): jnp.concatenate(lax.all_gather(rounded, 'row'), axis=1)]
    dot_general x1, matrix products: 4.22 us -> 2.07 us  [on_device(): jnp.einsum('qar,qbr->ab', rounded, jnp.concatenate(lax.all_gather(rounded...]
where the time goes in v1:
time: 167 us; the launch traced here: 166 us
  waiting for transfers between devices  92.2 us (55%)
  blocking collectives  26.8 us (16%)
  local copies, waits for them, and re-layouts  22.1 us (13%)
  between operations  13.5 us (8%)
  matrix products  5.93 us (4%)
  starting transfers between devices  4.3 us (3%)
    all_gather x1, waiting for transfers between devices, on_device(): lax.all_gather(rounded, 'row')  73.9 us
    reduce_scatter x1, waiting for transfers between devices, on_device(): lax.psum_scatter(partial_gram, 'col', scatter_dimension=1, tiled=True)  18.3 us
    all_gather x1, blocking collectives, on_device(): whole_factor = lax.all_gather(basis_two, 'col', axis=0, tiled=True)  15.6 us
    all_to_all x1, blocking collectives, on_device(): lax.all_to_all(full.astype(jnp.bfloat16), 'col', split_axis=0, concat_axi...  11.2 us
    unnamed x8, local copies, waits for them, and re-layouts  6.55 us
    all_to_all x2, local copies, waits for them, and re-layouts, on_device(): lax.all_to_all(inner, 'col', split_axis=2, concat_axis=1, tiled=True)  6.45 us
    all_to_all x1, starting transfers between devices, on_device(): lax.all_to_all(inner, 'col', split_axis=2, concat_axis=1, tiled=True)  4.26 us
    dot_general x1, matrix products, on_device(): jnp.dot(snapshot.reshape(cells_one * cells_two, cells_three), basis_three...  3.44 us
  transfers between devices with their start and end apart: 3, of which 2 were waited for; matrix products, arithmetic and copies ran while one was open for 0% of the time, Pallas kernels for 0%

profile of v1, /device:TPU:0, one launch (start us, length us, event | category | flops | bytes accessed | tf_op | source)
XLA Modules:
  0.0 166.2 jit_solution(14138731926800955195)
XLA Ops:
  6.5 0.9 copy-done
  7.4 3.4 %convolution_convert_fusion = bf16[4096,128]{1,0:T(8,128)(2,1)S(1)} fusion(bf16[4096,512]{1,0:T(8,128)(2,1)} %bitcast.35, bf16[512,128]{1,0:T(8,128)(2,1)S(1)} %copy-done), kind=kOutput, calls=%fused_computation | convolution fusion | flops 537395200 | bytes 5373952 | tf_op jit(solution)/shard_map/dot_general | solution.py:11
  10.9 3.0 %copy.23 = bf16[64,64,128]{1,0,2:T(8,128)(2,1)S(1)} copy(bf16[64,64,128]{2,1,0:T(8,128)(2,1)S(1)} %bitcast.36) | data formatting | bytes 2097152 | tf_op jit(solution)/shard_map/reshape | solution.py:16
  13.9 2.6 %reshape.19 = bf16[4,2,65536]{2,1,0:T(2,128)(2,1)} reshape(bf16[128,64,64]{2,1,0:T(8,128)(2,1)S(1)} %bitcast.33) | data formatting | bytes 2097152
  16.5 4.3 %all-to-all-start = ((bf16[4,2,65536]{2,1,0:T(2,128)(2,1)}), bf16[4,2,65536]{2,1,0:T(2,128)(2,1)S(1)}, u32[]{:S(2)}, u32[]{:S(2)}) async-start(bf16[4,2,65536]{2,1,0:T(2,128)(2,1)} %reshape.19), calls=%async_computation | async-start | bytes 2097152 | tf_op jit(solution)/shard_map/all_to_all | solution.py:17
  20.8 15.6 %all_gather.9 = bf16[256,128]{1,0:T(8,128)(2,1)S(1)} all-gather(bf16[64,128]{1,0:T(8,128)(2,1)S(1)} %copy-done.1), channel_id=1, replica_groups=mesh['row'=8,'col'=4] {'col'}, dimensions={0}, use_global_device_ids=true | all-gather | bytes 81920 | tf_op jit(solution)/shard_map/all_gather | solution.py:18
  36.4 1.4 reshape.20
  37.8 3.0 %copy.25 = bf16[64,4,64,32]{2,1,3,0:T(4,128)(2,1)} copy(bf16[64,4,64,32]{2,0,3,1:T(8,128)(2,1)S(1)} %bitcast.34) | data formatting | bytes 2097152 | tf_op jit(solution)/shard_map/all_to_all | solution.py:17
  40.8 3.5 %all_to_all.29 = bf16[64,256,32]{1,2,0:T(8,128)(2,1)S(1)} reshape(bf16[64,4,64,32]{2,1,3,0:T(4,128)(2,1)} %copy.25) | data formatting | bytes 2097152 | tf_op jit(solution)/shard_map/all_to_all | solution.py:17
  44.3 0.4 fusion
  44.7 1.7 %copy.26 = bf16[128,64,32]{1,2,0:T(8,128)(2,1)S(1)} copy(bf16[128,64,32]{0,2,1:T(8,128)(2,1)S(1)} %fusion) | data formatting | bytes 1048576 | tf_op jit(solution)/shard_map/convert_element_type | solution.py:21
  46.4 0.9 reshape.21
  47.3 11.2 %all_to_all.36 = bf16[4,2,32768]{2,1,0:T(2,128)(2,1)S(1)} all-to-all(bf16[4,2,32768]{2,1,0:T(2,128)(2,1)S(1)} %reshape.21), channel_id=1, replica_groups=mesh['row'=8,'col'=4] {'col'}, dimensions={0} | all-to-all | bytes 1048576 | tf_op jit(solution)/shard_map/all_to_all | solution.py:20
  58.5 0.7 reshape.22
  59.2 0.1 copy.27
  59.4 1.1 copy.29
  60.5 0.0 all-gather.2.cloned.1.call-update
  60.5 0.0 reduce-scatter.2.cloned.1.call-start
  60.6 73.9 %all-gather.2.cloned.1.call-done = bf16[8,32,64,128]{3,2,1,0:T(8,128)(2,1)} async-done(((bf16[1,32,64,128]{3,2,1,0:T(8,128)(2,1)}), bf16[8,32,64,128]{3,2,1,0:T(8,128)(2,1)}) %all-gather.2.cloned.1.call-update) | async-done | bytes 4194320 | tf_op jit(solution)/shard_map/all_gather | solution.py:26
  134.5 3.1 %copy.30 = bf16[32,8,64,128]{3,2,1,0:T(8,128)(2,1)S(1)} copy(bf16[32,8,64,128]{3,2,0,1:T(8,128)(2,1)} %bitcast.38) | data formatting | bytes 8388608 | tf_op jit(solution)/shard_map/reshape | solution.py:26
  137.6 2.1 %convolution_bitcast_fusion = f32[64,512]{1,0:T(8,128)} fusion(bf16[32,64,128]{1,2,0:T(8,128)(2,1)S(1)} %bitcast.32, bf16[32,512,128]{2,1,0:T(8,128)(2,1)S(1)} %bitcast.30), kind=kOutput, calls=%fused_computation.3 | convolution fusion | flops 268435456 | bytes 4849664 | tf_op jit(solution)/shard_map/qar,qbr->ab/dot_general | solution.py:23
  139.7 0.0 reduce-scatter.2.cloned.1.call-update
  139.7 18.3 %reduce-scatter.2.cloned.1.call-done = f32[64,128]{1,0:T(8,128)} async-done(((f32[64,512]{1,0:T(8,128)}), f32[64,128]{1,0:T(8,128)}) %reduce-scatter.2.cloned.1.call-update) | async-done | bytes 32784 | tf_op jit(solution)/shard_map/reduce_scatter | solution.py:29
  158.0 1.4 broadcast_multiply_fusion
  (5 shorter events, 0.0 us)
Async XLA Ops:
  6.5 0.9 copy-start
  10.9 9.9 %copy-start.1 = (bf16[64,128]{1,0:T(8,128)(2,1)S(1)}, bf16[64,128]{1,0:T(8,128)(2,1)}, u32[]{:S(2)}) copy-start(bf16[64,128]{1,0:T(8,128)(2,1)} %param.4) | copy-start | bytes 49156
  16.5 19.9 %all-to-all-start = ((bf16[4,2,65536]{2,1,0:T(2,128)(2,1)}), bf16[4,2,65536]{2,1,0:T(2,128)(2,1)S(1)}, u32[]{:S(2)}, u32[]{:S(2)}) async-start(bf16[4,2,65536]{2,1,0:T(2,128)(2,1)} %reshape.19), calls=%async_computation | async-start | bytes 2097152 | tf_op jit(solution)/shard_map/all_to_all | solution.py:17
  20.8 113.7 %all-gather.2.cloned.1.call-start = ((), (), s32[]{:S(2)}) async-start(), calls=%async_computation.3 | async-start | bytes 4718592 | tf_op jit(solution)/shard_map/all_gather | solution.py:26
  60.5 97.5 %reduce-scatter.2.cloned.1.call-start = ((), (), s32[]{:S(2)}) async-start(), calls=%async_computation.4 | async-start | bytes 163840 | tf_op jit(solution)/shard_map/reduce_scatter | solution.py:29
Sparse Core Ops, SparseCore 0:
  60.6 73.7 all-gather.1
  139.8 18.1 reduce-scatter.1
